TPU v7x, 32 devices: a whole 2x2x4 slice. The times are simulated.
32 devices in a mesh: row: 2 (over x), col: 16 (over z, y, core).
Axes of the slice: x: 2, y: 2, z: 4, core: 2. Of those that a mesh axis runs over, the one named last changes fastest.
Arguments:
- upper_a: float32 [8, 2, 256, 16, 256], P(None, 'row', None, 'col'), may hold values from -0.375 to 0.375
- upper_b: float32 [8, 2, 256, 16, 256], P(None, 'row', None, 'col'), may hold values from -0.375 to 0.375
- right_side: float32 [8, 2, 256, 16, 256], P(None, 'row', None, 'col'), may hold values from -6 to 6
- vectors_a: float32 [8, 2, 256, 256], P(None, 'row'), may hold values from -0.375 to 0.375
- inverse_a: float32 [8, 2, 256, 256], P(None, 'row'), may hold values from -0.375 to 0.375
- values_a: float32 [8, 2, 256], P(None, 'row'), may hold values from 0.5 to 2
- vectors_b: float32 [16, 256, 256], P('col'), may hold values from -0.375 to 0.375
- inverse_b: float32 [16, 256, 256], P('col'), may hold values from -0.375 to 0.375
- values_b: float32 [16, 256], P('col'), may hold values from 0.5 to 2
Outputs:
- solved: float32 [8, 2, 256, 16, 256], P(None, 'row', None, 'col')
All inputs are finite; a program needn't handle non-finite values.
Results may differ from a plain program's by a relative error of at most 0.0001.
Values sent between devices are 32-bit elements; how exact they have to be, the bound alone decides.
A program may use at most 64 MiB of HBM per device.

v0:
```python
import jax
import jax.numpy as jnp
from jax import lax
from jax.sharding import PartitionSpec as P

FRONTS = 4
EXACT = lax.Precision.HIGHEST


def passed_along(value, axis, by):
    length = lax.axis_size(axis)
    pairs = [(i, i + by) for i in range(length) if 0 <= i + by < length]
    return lax.ppermute(value, axis, pairs)


def shifted(value, axis, steps):
    count = lax.axis_size(axis)
    pairs = [(source, (source + steps) % count) for source in range(count)]
    return lax.ppermute(value, axis, pairs)


def spread(value, axis, root):
    mine = lax.axis_index(axis) == root
    return lax.psum(jnp.where(mine, value, jnp.zeros_like(value)), axis)


def matmul(former, latter):
    return jnp.dot(former, latter, precision=EXACT, preferred_element_type=jnp.float32)


def diagonal_solve(residual, vectors_a, inverse_a, values_a, vectors_b, inverse_b, values_b):
    rotated = matmul(matmul(inverse_a, residual), vectors_b)
    scaled = rotated / (values_a[:, None] + values_b[None, :])
    return matmul(matmul(vectors_a, scaled), inverse_b)


def body(
    upper_a, upper_b, right_side, vectors_a, inverse_a, values_a, vectors_b, inverse_b, values_b
):
    row_count = lax.axis_size("row")
    col_count = lax.axis_size("col")
    row_pos = lax.axis_index("row")
    col_pos = lax.axis_index("col")
    local_blocks = right_side.shape[0]
    block_size = right_side.shape[2]
    square = (local_blocks, block_size, block_size)
    panel_a = upper_a.reshape(square)
    panel_b = upper_b.reshape(square)
    work = right_side.reshape(square)
    left_vectors = vectors_a.reshape(square)
    left_inverse = inverse_a.reshape(square)
    left_values = values_a.reshape(local_blocks, block_size)
    right_vectors = vectors_b.reshape(block_size, block_size)
    right_inverse = inverse_b.reshape(block_size, block_size)
    right_values = values_b.reshape(block_size)
    block_ids = jnp.arange(local_blocks, dtype=jnp.int32)
    global_rows = block_ids * row_count + row_pos
    offsets = list(range(-1, FRONTS - 1))
    moved_upper = {}
    for offset in offsets:
        if offset == 0:
            moved_upper[offset] = panel_a
        else:
            moved_upper[offset] = passed_along(panel_a, "col", offset)
    zero_block = jnp.zeros((1, block_size, block_size), jnp.float32)
    moved_lower = {}
    for offset in offsets:
        if offset % row_count == 0:
            arrived = panel_b
        else:
            arrived = shifted(panel_b, "row", -offset)
        block_carry = jnp.floor_divide(row_pos + offset, row_count)
        padded = jnp.concatenate([zero_block, arrived, zero_block], axis=0)
        moved_lower[offset] = lax.dynamic_slice_in_dim(padded, 1 + block_carry, local_blocks, 0)
    for offset in offsets:
        target = col_pos - offset
        slot_index = jnp.floor_divide(target - row_pos, row_count)
        present = (
            (jnp.remainder(target - row_pos, row_count) == 0) & (target >= 0) & (target < col_count)
        )
        picked = jnp.clip(slot_index, 0, local_blocks - 1)
        residual = lax.dynamic_index_in_dim(work, picked, 0, keepdims=False)
        solved = diagonal_solve(
            residual,
            lax.dynamic_index_in_dim(left_vectors, picked, 0, keepdims=False),
            lax.dynamic_index_in_dim(left_inverse, picked, 0, keepdims=False),
            lax.dynamic_index_in_dim(left_values, picked, 0, keepdims=False),
            right_vectors,
            right_inverse,
            right_values,
        )
        on_front = (block_ids == slot_index) & present
        work = jnp.where(on_front[:, None, None], solved[None], work)
        column_block = spread(solved, "row", jnp.remainder(target, row_count))
        upper_term = jnp.einsum("qab,bc->qac", moved_upper[offset], column_block, precision=EXACT)
        slot_blocks = jnp.where(on_front[:, None, None], solved[None], jnp.zeros_like(work))
        row_solved = lax.psum(slot_blocks, "col")
        lower_term = jnp.einsum("qab,qbc->qac", row_solved, moved_lower[offset], precision=EXACT)
        pending = col_pos - global_rows > offset
        work = jnp.where(pending[:, None, None], work - (upper_term + lower_term), work)
    return work.reshape(right_side.shape)


def solution(mesh):
    return jax.shard_map(
        body,
        mesh=mesh,
        in_specs=(
            P(None, "row", None, "col", None),
            P(None, "row", None, "col", None),
            P(None, "row", None, "col", None),
            P(None, "row", None, None),
            P(None, "row", None, None),
            P(None, "row", None),
            P("col", None, None),
            P("col", None, None),
            P("col", None),
        ),
        out_specs=P(None, "row", None, "col", None),
        check_vma=False,
    )
```

profile of v0, /device:TPU:0, one launch (start us, length us, event | category | flops | bytes accessed | tf_op | source)
XLA Modules:
  0.0 592.5 jit_solution(1330975827765755095)
XLA Ops:
  6.5 3.2 copy.54
  9.7 3.0 collective-permute-start.1
  12.7 1.5 copy.55
  14.3 1.4 collective-permute-start
  15.8 1.1 constant_dynamic-slice_fusion.4
  17.0 0.4 fusion.13
  17.4 0.4 convolution_divide_fusion.3
  17.8 1.3 fusion.41
  19.1 1.1 broadcast_select_fusion.7
  20.5 1.7 broadcast_select_fusion.3
  22.5 6.0 %copy.11 = f32[8,1,256,1,256]{2,4,0,3,1:T(8,128)} copy(f32[8,1,256,1,256]{4,3,2,1,0:T(1,128)} %param.11) | data formatting | bytes 4194304 | tf_op args[2]
  28.6 35.7 %collective-permute-done.1 = f32[8,256,256]{2,1,0:T(8,128)} collective-permute-done((f32[8,256,256]{2,1,0:T(8,128)}, f32[8,256,256]{2,1,0:T(8,128)}, u32[]{:S(2)}, u32[]{:S(2)}) %collective-permute-start.1) | collective-permute-done | bytes 2097184 | tf_op jit(solution)/shard_map/ppermute | solution.py:19
  64.3 5.4 pad_maximum_fusion
  69.7 6.5 %fusion.26 = f32[256,8,256]{2,0,1:T(8,128)} fusion(f32[8,256,256]{2,1,0:T(8,128)} %collective-permute-done, f32[256,256]{1,0:T(8,128)} %all-reduce.9.cloned.1.call-done), kind=kOutput, calls=%fused_computation.45 | convolution fusion | flops 1610612736 | bytes 4456448 | tf_op jit(solution)/shard_map/qab,bc->qac/dot_general | solution.py:95
  76.2 77.0 %all-reduce.11.cloned.1.call-done = f32[8,256,256]{1,2,0:T(8,128)} async-done(((f32[8,256,256]{1,2,0:T(8,128)}), f32[8,256,256]{1,2,0:T(8,128)}) %all-reduce.11.cloned.1.call-update) | async-done | bytes 2097168 | tf_op jit(solution)/shard_map/psum | solution.py:97
  153.2 7.2 %subtract_select_fusion.3 = f32[8,256,256]{1,2,0:T(8,128)S(1)} fusion(f32[256,8,256]{2,0,1:T(8,128)} %fusion.26, f32[8,1,256,1,256]{2,4,0,3,1:T(8,128)} %copy.11, f32[8,256,256]{1,2,0:T(8,128)} %all-reduce.11.cloned.1.call-done, f32[10,256,256]{2,1,0:T(8,128)} %get-tuple-element.8, s32[]{:T(128)S(6)} %select_n.168, f32[256,256]{0,1:T(8,128)S(1)} %copy.10, ...), kind=kOutput, calls=%fused_computation.7 | convolution fusion | flops 1612709888 | bytes 10747924 | tf_op jit(solution)/shard_map/qab,qbc->qac/dot_general | solution.py:98
  160.4 1.3 copy-done.2
  161.7 0.4 fusion.24
  162.5 1.3 fusion.44
  163.9 1.1 broadcast_select_fusion.6
  165.1 1.7 broadcast_select_fusion.2
  166.9 2.7 collective-permute-start.2
  169.6 0.6 all-reduce.17.cloned.1.call-start
  170.2 98.3 %all-reduce.15.cloned.1.call-done = f32[8,256,256]{1,2,0:T(8,128)} async-done(((f32[8,256,256]{1,2,0:T(8,128)}), f32[8,256,256]{1,2,0:T(8,128)}) %all-reduce.15.cloned.1.call-update) | async-done | bytes 2097168 | tf_op jit(solution)/shard_map/psum | solution.py:97
  268.5 7.2 %fusion.5 = f32[8,256,256]{1,2,0:T(8,128)} fusion(f32[8,256,256]{1,2,0:T(8,128)} %all-reduce.15.cloned.1.call-done, f32[10,256,256]{2,1,0:T(8,128)} %get-tuple-element.7, s32[]{:T(128)S(6)} %select_n.176), kind=kOutput, calls=%fused_computation.20 | convolution fusion | flops 1610612736 | bytes 6291460 | tf_op jit(solution)/shard_map/qab,qbc->qac/dot_general | solution.py:98
  275.7 17.7 %all-reduce.13.cloned.1.call-done = f32[256,256]{1,0:T(8,128)} async-done(((f32[256,256]{1,0:T(8,128)}), f32[256,256]{1,0:T(8,128)}) %all-reduce.13.cloned.1.call-update) | async-done | bytes 262160 | tf_op jit(solution)/shard_map/psum | solution.py:24
  293.4 6.7 %subtract_select_fusion.2 = f32[8,256,256]{1,2,0:T(8,128)S(1)} fusion(f32[8,256,256]{1,2,0:T(8,128)} %fusion.5, f32[8,256,256]{1,2,0:T(8,128)} %copy-done.2, f32[256,256]{0,1:T(8,128)S(1)} %copy.15, pred[8]{0:T(512)(128)(4,1)S(1)} %compare_and_fusion.1, pred[8]{0:T(512)(128)(4,1)S(1)} %get-tuple-element.14, f32[256,256]{1,0:T(8,128)} %all-reduce.13.cloned.1.call-done, ...), kind=kOutput, calls=%fused_computation.6 | convolution fusion | flops 1612709888 | bytes 8912912 | tf_op jit(solution)/shard_map/qab,bc->qac/dot_general | solution.py:95
  300.2 1.3 copy-done.1
  301.4 0.4 fusion.21
  302.3 1.3 fusion.47
  303.6 1.1 broadcast_select_fusion.5
  304.9 1.6 broadcast_select_fusion.1
  306.5 4.9 collective-permute-start.3
  311.5 16.8 %all-reduce.17.cloned.1.call-done = f32[256,256]{1,0:T(8,128)} async-done(((f32[256,256]{1,0:T(8,128)}), f32[256,256]{1,0:T(8,128)}) %all-reduce.17.cloned.1.call-update) | async-done | bytes 262160 | tf_op jit(solution)/shard_map/psum | solution.py:24
  328.3 6.5 %fusion.19 = f32[256,8,256]{2,0,1:T(8,128)} fusion(f32[8,256,256]{2,1,0:T(8,128)} %collective-permute-done.2, f32[256,256]{1,0:T(8,128)} %all-reduce.17.cloned.1.call-done), kind=kOutput, calls=%fused_computation.38 | convolution fusion | flops 1610612736 | bytes 4456448 | tf_op jit(solution)/shard_map/qab,bc->qac/dot_general | solution.py:95
  334.8 100.3 %all-reduce.19.cloned.1.call-done = f32[8,256,256]{1,2,0:T(8,128)} async-done(((f32[8,256,256]{1,2,0:T(8,128)}), f32[8,256,256]{1,2,0:T(8,128)}) %all-reduce.19.cloned.1.call-update) | async-done | bytes 2097168 | tf_op jit(solution)/shard_map/psum | solution.py:97
  435.1 7.2 %subtract_select_fusion.1 = f32[8,256,256]{1,2,0:T(8,128)S(1)} fusion(f32[256,8,256]{2,0,1:T(8,128)} %fusion.19, f32[8,256,256]{1,2,0:T(8,128)} %copy-done.1, f32[8,256,256]{1,2,0:T(8,128)} %all-reduce.19.cloned.1.call-done, f32[10,256,256]{2,1,0:T(8,128)} %get-tuple-element.8, s32[]{:T(128)S(6)} %select_n.184, f32[256,256]{0,1:T(8,128)S(1)} %copy.19, ...), kind=kOutput, calls=%fused_computation.5 | convolution fusion | flops 1612709888 | bytes 10747924 | tf_op jit(solution)/shard_map/qab,qbc->qac/dot_general | solution.py:98
  442.3 1.3 copy-done.3
  443.7 0.4 fusion.17
  444.5 1.3 fusion.50
  445.8 1.1 broadcast_select_fusion.4
  447.0 1.5 broadcast_select_fusion
  448.9 0.5 all-reduce.21.cloned.1.call-update
  449.3 97.0 %all-reduce.23.cloned.1.call-done = f32[8,256,256]{1,2,0:T(8,128)} async-done(((f32[8,256,256]{1,2,0:T(8,128)}), f32[8,256,256]{1,2,0:T(8,128)}) %all-reduce.23.cloned.1.call-update) | async-done | bytes 2097168 | tf_op jit(solution)/shard_map/psum | solution.py:97
  546.4 7.0 %fusion.1 = f32[8,256,256]{1,2,0:T(8,128)} fusion(f32[8,256,256]{1,2,0:T(8,128)} %all-reduce.23.cloned.1.call-done, f32[10,256,256]{2,1,0:T(8,128)} %get-tuple-element.7, s32[]{:T(128)S(6)} %select_n.192), kind=kOutput, calls=%fused_computation.16 | convolution fusion | flops 1610612736 | bytes 6291460 | tf_op jit(solution)/shard_map/qab,qbc->qac/dot_general | solution.py:98
  553.4 18.0 %all-reduce.21.cloned.1.call-done = f32[256,256]{1,0:T(8,128)} async-done(((f32[256,256]{1,0:T(8,128)}), f32[256,256]{1,0:T(8,128)}) %all-reduce.21.cloned.1.call-update) | async-done | bytes 262160 | tf_op jit(solution)/shard_map/psum | solution.py:24
  571.5 8.0 %fusion = f32[8,1,256,1,256]{2,4,0,3,1:T(8,128)} fusion(f32[8,256,256]{1,2,0:T(8,128)} %fusion.1, f32[8,256,256]{1,2,0:T(8,128)} %copy-done.3, f32[8,256,256]{2,1,0:T(8,128)} %collective-permute-done.3, f32[256,256]{0,1:T(8,128)S(1)} %copy.23, pred[8]{0:T(512)(128)(4,1)S(1)} %compare_and_fusion.3, pred[8]{0:T(512)(128)(4,1)S(1)} %get-tuple-element.5, ...), kind=kOutput, calls=%fused_computation.8 | convolution fusion | flops 1612709888 | bytes 8912912 | tf_op jit(solution)/shard_map/qab,bc->qac/dot_general | solution.py:95
  579.4 6.0 %copy.27 = f32[8,1,256,1,256]{4,3,2,1,0:T(1,128)} copy(f32[8,1,256,1,256]{2,4,0,3,1:T(8,128)} %fusion) | data formatting | bytes 4194304 | tf_op jit(solution)/shard_map/reshape | solution.py:101
  (48 shorter events, 2.6 us)
Async XLA Ops:
  6.5 10.4 %copy-start = (f32[8,1,256,256]{3,2,1,0:T(8,128)S(1)}, f32[8,1,256,256]{3,2,1,0:T(8,128)}, u32[]{:S(2)}) copy-start(f32[8,1,256,256]{3,2,1,0:T(8,128)} %param.13) | copy-start | bytes 6291460
  6.5 63.1 %all-reduce.9.cloned.1.call-start = ((), (), s32[]{:S(2)}) async-start(), calls=%async_computation | async-start | bytes 524288 | tf_op jit(solution)/shard_map/psum | solution.py:24
  6.5 6.2 %copy-start.4 = (f32[8,1,256,1,256]{4,3,2,1,0:T(1,128)S(1)}, f32[8,1,256,1,256]{4,3,2,1,0:T(1,128)}, u32[]{:S(2)}) copy-start(f32[8,1,256,1,256]{4,3,2,1,0:T(1,128)} %param.9) | copy-start | bytes 6291460
  9.7 7.2 %copy-start.6 = (f32[8,1,256]{2,1,0:T(1,128)S(1)}, f32[8,1,256]{2,1,0:T(1,128)}, u32[]{:S(2)}) copy-start(f32[8,1,256]{2,1,0:T(1,128)} %param.14) | copy-start | bytes 24580
  9.7 7.6 %copy-start.7 = (f32[1,256,256]{2,1,0:T(8,128)S(1)}, f32[1,256,256]{2,1,0:T(8,128)}, u32[]{:S(2)}) copy-start(f32[1,256,256]{2,1,0:T(8,128)} %param.15) | copy-start | bytes 786436
  9.7 7.7 %copy-start.8 = (f32[1,256]{1,0:T(1,128)S(1)}, f32[1,256]{1,0:T(1,128)}, u32[]{:S(2)}) copy-start(f32[1,256]{1,0:T(1,128)} %param.17) | copy-start | bytes 3076
  9.7 54.5 %collective-permute-start.1 = (f32[8,256,256]{2,1,0:T(8,128)}, f32[8,256,256]{2,1,0:T(8,128)}, u32[]{:S(2)}, u32[]{:S(2)}) collective-permute-start(f32[8,256,256]{2,1,0:T(8,128)} %bitcast.125), channel_id=1, source_target_pairs={{0,16},{16,0},{1,17},{17,1},{2,18},{18,2},{3,19},{19,3},{4,20},{20... | collective-permute-start | bytes 6291464 | tf_op jit(solution)/shard_map/ppermute | solution.py:19
  14.3 4.9 copy-start.5
  14.3 55.4 %collective-permute-start = (f32[8,256,256]{2,1,0:T(8,128)}, f32[8,256,256]{2,1,0:T(8,128)}, u32[]{:S(2)}, u32[]{:S(2)}) collective-permute-start(f32[8,256,256]{2,1,0:T(8,128)} %bitcast.126), channel_id=1, source_target_pairs={{1,0},{2,1},{3,2},{4,3},{5,4},{6,5},{7,6},{8,7},{9,8},{10,9},{11,1... | collective-permute-start | bytes 6291464 | tf_op jit(solution)/shard_map/ppermute | solution.py:13
  20.2 132.9 %all-reduce.11.cloned.1.call-start = ((), (), s32[]{:S(2)}) async-start(), calls=%async_computation.1 | async-start | bytes 4194304 | tf_op jit(solution)/shard_map/psum | solution.py:97
  22.2 246.3 %all-reduce.15.cloned.1.call-start = ((), (), s32[]{:S(2)}) async-start(), calls=%async_computation.3 | async-start | bytes 4194304 | tf_op jit(solution)/shard_map/psum | solution.py:97
  160.4 1.4 copy-start.2
  166.8 126.6 %all-reduce.13.cloned.1.call-start = ((), (), s32[]{:S(2)}) async-start(), calls=%async_computation.2 | async-start | bytes 524288 | tf_op jit(solution)/shard_map/psum | solution.py:24
  166.9 144.6 %collective-permute-start.2 = (f32[8,256,256]{2,1,0:T(8,128)}, f32[8,256,256]{2,1,0:T(8,128)}, u32[]{:S(2)}, u32[]{:S(2)}) collective-permute-start(f32[8,256,256]{2,1,0:T(8,128)} %bitcast.126), channel_id=1, source_target_pairs={{0,1},{1,2},{2,3},{3,4},{4,5},{5,6},{6,7},{7,8},{8,9},{9,10},{10,1... | collective-permute-start | bytes 6291464 | tf_op jit(solution)/shard_map/ppermute | solution.py:13
  169.6 158.7 %all-reduce.17.cloned.1.call-start = ((), (), s32[]{:S(2)}) async-start(), calls=%async_computation.4 | async-start | bytes 524288 | tf_op jit(solution)/shard_map/psum | solution.py:24
  300.1 1.3 copy-start.1
  304.8 130.2 %all-reduce.19.cloned.1.call-start = ((), (), s32[]{:S(2)}) async-start(), calls=%async_computation.5 | async-start | bytes 4194304 | tf_op jit(solution)/shard_map/psum | solution.py:97
  306.5 239.9 %all-reduce.23.cloned.1.call-start = ((), (), s32[]{:S(2)}) async-start(), calls=%async_computation.7 | async-start | bytes 4194304 | tf_op jit(solution)/shard_map/psum | solution.py:97
  306.5 246.9 %collective-permute-start.3 = (f32[8,256,256]{2,1,0:T(8,128)}, f32[8,256,256]{2,1,0:T(8,128)}, u32[]{:S(2)}, u32[]{:S(2)}) collective-permute-start(f32[8,256,256]{2,1,0:T(8,128)} %bitcast.126), channel_id=1, source_target_pairs={{0,2},{1,3},{2,4},{3,5},{4,6},{5,7},{6,8},{7,9},{8,10},{9,11},{10,... | collective-permute-start | bytes 6291464 | tf_op jit(solution)/shard_map/ppermute | solution.py:13
  442.3 1.4 copy-start.3
  448.6 122.9 %all-reduce.21.cloned.1.call-start = ((), (), s32[]{:S(2)}) async-start(), calls=%async_computation.6 | async-start | bytes 524288 | tf_op jit(solution)/shard_map/psum | solution.py:24
Sparse Core Ops, SparseCore 0:
  20.4 31.0 all-reduce.8
  55.0 98.1 all-reduce.10
  166.9 101.5 all-reduce.14
  270.6 22.7 all-reduce.12
  305.0 23.2 all-reduce.16
  331.7 103.3 all-reduce.18
  448.7 97.6 all-reduce.22
  548.7 22.7 all-reduce.20
where the time goes:
time: 596 us; the launch traced here: 592 us
  waiting for transfers between devices  462 us (78%)
  matrix products  69 us (12%)
  local copies, waits for them, and re-layouts  22.5 us (4%)
  between operations  14.2 us (2%)
  starting transfers between devices  13.3 us (2%)
  other arithmetic  11.9 us (2%)
    psum x4, waiting for transfers between devices, body(): row_solved = lax.psum(slot_blocks, 'col')  373 us
    psum x4, waiting for transfers between devices, spread(): return lax.psum(jnp.where(mine, value, jnp.zeros_like(value)), axis)  52.6 us
    ppermute x1, waiting for transfers between devices, shifted(): return lax.ppermute(value, axis, pairs)  35.7 us
    dot_general x4, matrix products, body(): jnp.einsum('qab,qbc->qac', row_solved, moved_lower[offset], precision=EXACT)  28.6 us
    dot_general x4, matrix products, body(): jnp.einsum('qab,bc->qac', moved_upper[offset], column_block, precision=EX...  27.6 us
    unnamed x21, local copies, waits for them, and re-layouts  14.8 us
    dot_general x16, matrix products, matmul(): jnp.dot(former, latter, precision=EXACT, preferred_element_type=jnp.float32)  12.8 us
  transfers between devices with their start and end apart: 12, of which 8 were waited for; matrix products, arithmetic and copies ran while one was open for 12% of the time, Pallas kernels for 0%

commit v1 on v0

--- a/solution.py
+++ b/solution.py
@@ -21,7 +21,11 @@
 
 def spread(value, axis, root):
     mine = lax.axis_index(axis) == root
-    return lax.psum(jnp.where(mine, value, jnp.zeros_like(value)), axis)
+
+    def proceed_squares_for(q_in):
+        return jnp.sum(jax.lax.all_gather(q_in, axis_name=axis), 0)
+
+    return proceed_squares_for(jnp.where(mine, value, jnp.zeros_like(value)))
 
 
 def matmul(former, latter):

time: 596 us -> 499 us (0.84)
  waiting for transfers between devices: 462 us -> 305 us
  blocking collectives: 0 us -> 71.8 us
  matrix products: 69 us -> 59.7 us
    all_gather x0 -> x4, blocking collectives: none -> 71.8 us  [proceed_squares_for(): return jnp.sum(jax.lax.all_gather(q_in, axis_name=axis), 0)]
    psum x4, waiting for transfers between devices: 373 us -> 304 us  [body(): row_solved = lax.psum(slot_blocks, 'col')]
    psum x4 -> x0, waiting for transfers between devices: 52.6 us -> none  [spread(): return lax.psum(jnp.where(mine, value, jnp.zeros_like(value)), axis)]
    ppermute x1, waiting for transfers between devices: 35.7 us -> 0.01 us  [shifted(): return lax.ppermute(value, axis, pairs)]
    unnamed x21 -> x33, local copies, waits for them, and re-layouts: 14.8 us -> 14.8 us
  transfers between devices with their start and end apart: 12 -> 8, of which waited for: 8 -> 4; matrix products, arithmetic and copies ran while one was open for 12% -> 13% of each run, Pallas kernels for 0% -> 0%
where the time goes in v1:
time: 499 us; the launch traced here: 496 us
  waiting for transfers between devices  305 us (61%)
  blocking collectives  71.8 us (14%)
  matrix products  59.7 us (12%)
  local copies, waits for them, and re-layouts  22.5 us (5%)
  between operations  13.9 us (3%)
  other arithmetic  12 us (2%)
  starting transfers between devices  11.6 us (2%)
    psum x4, waiting for transfers between devices, body(): row_solved = lax.psum(slot_blocks, 'col')  304 us
    all_gather x4, blocking collectives, proceed_squares_for(): return jnp.sum(jax.lax.all_gather(q_in, axis_name=axis), 0)  71.8 us
    dot_general x4, matrix products, body(): jnp.einsum('qab,qbc->qac', row_solved, moved_lower[offset], precision=EXACT)  26.2 us
    dot_general x4, matrix products, body(): jnp.einsum('qab,bc->qac', moved_upper[offset], column_block, precision=EX...  23.5 us
    unnamed x33, local copies, waits for them, and re-layouts  14.8 us
    dot_general x16, matrix products, matmul(): jnp.dot(former, latter, precision=EXACT, preferred_element_type=jnp.float32)  9.98 us
  transfers between devices with their start and end apart: 8, of which 4 were waited for; matrix products, arithmetic and copies ran while one was open for 13% of the time, Pallas kernels for 0%

profile of v1, /device:TPU:0, one launch (start us, length us, event | category | flops | bytes accessed | tf_op | source)
XLA Modules:
  0.0 496.1 jit_solution(17231671994000134515)
XLA Ops:
  6.5 3.2 copy.69
  9.7 1.4 collective-permute-start
  11.2 1.5 copy.68
  12.7 3.0 collective-permute-start.1
  15.7 1.1 constant_dynamic-slice_fusion.4
  17.4 0.4 convolution_divide_fusion.3
  17.8 1.3 fusion.41
  19.1 0.4 broadcast_select_fusion.7
  19.7 1.7 broadcast_select_fusion.3
  21.4 46.1 %all-gather = f32[512,256]{1,0:T(8,128)S(1)} all-gather(f32[256,256]{1,0:T(8,128)S(1)} %get-tuple-element.16), channel_id=2, replica_groups=mesh['row'=2,'col'=16] {'row'}, dimensions={0}, use_global_device_ids=true | all-gather | bytes 786432 | tf_op jit(solution)/shard_map/all_gather | solution.py:26
  67.6 6.0 %copy.25 = f32[8,1,256,1,256]{2,4,0,3,1:T(8,128)} copy(f32[8,1,256,1,256]{4,3,2,1,0:T(1,128)} %param.11) | data formatting | bytes 4194304 | tf_op args[2]
  73.7 5.3 %pad_maximum_fusion = (f32[10,256,256]{2,1,0:T(8,128)}, f32[10,256,256]{2,1,0:T(8,128)}) fusion(f32[1,256,256]{2,1,0:T(8,128)S(1)} %broadcast_in_dim.129, f32[8,256,256]{2,1,0:T(8,128)} %bitcast.129, f32[8,256,256]{2,1,0:T(8,128)} %collective-permute-done.1), kind=kLoop, calls=%fused_computation | loop fusion | flops 2621440 | bytes 9699328 | tf_op jit(solution)/shard_map/concatenate | solution.py:77
  79.0 6.4 %fusion.26 = f32[256,8,256]{2,0,1:T(8,128)} fusion(f32[8,256,256]{2,1,0:T(8,128)} %collective-permute-done, f32[256,256]{1,0:T(8,128)S(1)} %reduce_sum.36), kind=kOutput, calls=%fused_computation.45 | convolution fusion | flops 1610612736 | bytes 4456448 | tf_op jit(solution)/shard_map/qab,bc->qac/dot_general | solution.py:99
  85.4 37.8 %all-reduce.5.cloned.1.call-done = f32[8,256,256]{1,2,0:T(8,128)} async-done(((f32[8,256,256]{1,2,0:T(8,128)}), f32[8,256,256]{1,2,0:T(8,128)}) %all-reduce.5.cloned.1.call-update) | async-done | bytes 2097168 | tf_op jit(solution)/shard_map/psum | solution.py:101
  123.2 7.2 %subtract_select_fusion.3 = f32[8,256,256]{1,2,0:T(8,128)S(1)} fusion(f32[256,8,256]{2,0,1:T(8,128)} %fusion.26, f32[8,1,256,1,256]{2,4,0,3,1:T(8,128)} %copy.25, f32[8,256,256]{1,2,0:T(8,128)} %all-reduce.5.cloned.1.call-done, f32[10,256,256]{2,1,0:T(8,128)} %get-tuple-element.8, s32[]{:T(128)S(6)} %select_n.168, f32[256,256]{0,1:T(8,128)S(1)} %copy.24, ...), kind=kOutput, calls=%fused_computation.7 | convolution fusion | flops 1612709888 | bytes 10747924 | tf_op jit(solution)/shard_map/qab,qbc->qac/dot_general | solution.py:102
  130.4 1.3 copy-done.2
  131.8 0.4 fusion.24
  132.2 0.4 convolution_divide_fusion.2
  132.6 1.3 fusion.44
  133.9 0.4 broadcast_select_fusion.6
  134.5 1.7 broadcast_select_fusion.2
  136.2 2.7 collective-permute-start.2
  139.0 9.9 %all-gather.1 = f32[512,256]{1,0:T(8,128)S(1)} all-gather(f32[256,256]{1,0:T(8,128)S(1)} %get-tuple-element.18), channel_id=3, replica_groups=mesh['row'=2,'col'=16] {'row'}, dimensions={0}, use_global_device_ids=true | all-gather | bytes 786432 | tf_op jit(solution)/shard_map/all_gather | solution.py:26
  148.9 89.0 %all-reduce.7.cloned.1.call-done = f32[8,256,256]{1,2,0:T(8,128)} async-done(((f32[8,256,256]{1,2,0:T(8,128)}), f32[8,256,256]{1,2,0:T(8,128)}) %all-reduce.7.cloned.1.call-update) | async-done | bytes 2097168 | tf_op jit(solution)/shard_map/psum | solution.py:101
  237.9 5.9 %fusion.5 = f32[8,256,256]{1,2,0:T(8,128)S(1)} fusion(f32[8,256,256]{1,2,0:T(8,128)} %all-reduce.7.cloned.1.call-done, f32[10,256,256]{2,1,0:T(8,128)} %get-tuple-element.7, s32[]{:T(128)S(6)} %select_n.176), kind=kOutput, calls=%fused_computation.20 | convolution fusion | flops 1610612736 | bytes 6291460 | tf_op jit(solution)/shard_map/qab,qbc->qac/dot_general | solution.py:102
  243.8 3.9 subtract_select_fusion.2
  247.8 1.3 copy-done.1
  249.1 0.4 fusion.21
  249.5 0.4 convolution_divide_fusion.1
  249.9 1.3 fusion.47
  251.2 0.4 broadcast_select_fusion.5
  251.7 1.6 broadcast_select_fusion.1
  253.4 4.4 collective-permute-start.3
  257.8 7.4 %all-gather.2 = f32[512,256]{1,0:T(8,128)S(1)} all-gather(f32[256,256]{1,0:T(8,128)S(1)} %get-tuple-element.20), channel_id=4, replica_groups=mesh['row'=2,'col'=16] {'row'}, dimensions={0}, use_global_device_ids=true | all-gather | bytes 786432 | tf_op jit(solution)/shard_map/all_gather | solution.py:26
  265.3 6.4 %fusion.19 = f32[256,8,256]{2,0,1:T(8,128)} fusion(f32[8,256,256]{2,1,0:T(8,128)} %collective-permute-done.2, f32[256,256]{1,0:T(8,128)S(1)} %reduce_sum.38), kind=kOutput, calls=%fused_computation.38 | convolution fusion | flops 1610612736 | bytes 4456448 | tf_op jit(solution)/shard_map/qab,bc->qac/dot_general | solution.py:99
  271.6 88.3 %all-reduce.9.cloned.1.call-done = f32[8,256,256]{1,2,0:T(8,128)} async-done(((f32[8,256,256]{1,2,0:T(8,128)}), f32[8,256,256]{1,2,0:T(8,128)}) %all-reduce.9.cloned.1.call-update) | async-done | bytes 2097168 | tf_op jit(solution)/shard_map/psum | solution.py:101
  360.0 7.2 %subtract_select_fusion.1 = f32[8,256,256]{1,2,0:T(8,128)S(1)} fusion(f32[256,8,256]{2,0,1:T(8,128)} %fusion.19, f32[8,256,256]{1,2,0:T(8,128)} %copy-done.1, f32[8,256,256]{1,2,0:T(8,128)} %all-reduce.9.cloned.1.call-done, f32[10,256,256]{2,1,0:T(8,128)} %get-tuple-element.8, s32[]{:T(128)S(6)} %select_n.184, f32[256,256]{0,1:T(8,128)S(1)} %copy.33, ...), kind=kOutput, calls=%fused_computation.5 | convolution fusion | flops 1612709888 | bytes 10747924 | tf_op jit(solution)/shard_map/qab,qbc->qac/dot_general | solution.py:102
  367.2 1.3 copy-done.4
  368.6 0.4 fusion.17
  369.0 0.4 convolution_divide_fusion
  369.4 1.3 fusion.50
  370.7 0.4 broadcast_select_fusion.4
  371.2 1.6 broadcast_select_fusion
  372.8 8.3 %all-gather.3 = f32[512,256]{1,0:T(8,128)S(1)} all-gather(f32[256,256]{1,0:T(8,128)S(1)} %get-tuple-element.22), channel_id=5, replica_groups=mesh['row'=2,'col'=16] {'row'}, dimensions={0}, use_global_device_ids=true | all-gather | bytes 786432 | tf_op jit(solution)/shard_map/all_gather | solution.py:26
  381.2 89.4 %all-reduce.11.cloned.1.call-done = f32[8,256,256]{1,2,0:T(8,128)} async-done(((f32[8,256,256]{1,2,0:T(8,128)}), f32[8,256,256]{1,2,0:T(8,128)}) %all-reduce.11.cloned.1.call-update) | async-done | bytes 2097168 | tf_op jit(solution)/shard_map/psum | solution.py:101
  470.6 5.9 %fusion.1 = f32[8,256,256]{1,2,0:T(8,128)S(1)} fusion(f32[8,256,256]{1,2,0:T(8,128)} %all-reduce.11.cloned.1.call-done, f32[10,256,256]{2,1,0:T(8,128)} %get-tuple-element.7, s32[]{:T(128)S(6)} %select_n.192), kind=kOutput, calls=%fused_computation.16 | convolution fusion | flops 1610612736 | bytes 6291460 | tf_op jit(solution)/shard_map/qab,qbc->qac/dot_general | solution.py:102
  476.5 6.8 %fusion = f32[8,1,256,1,256]{2,4,0,3,1:T(8,128)} fusion(f32[8,256,256]{1,2,0:T(8,128)S(1)} %fusion.1, f32[8,256,256]{1,2,0:T(8,128)S(1)} %copy-done.5, f32[8,256,256]{2,1,0:T(8,128)} %collective-permute-done.3, f32[256,256]{0,1:T(8,128)S(1)} %copy.37, pred[8]{0:T(512)(128)(4,1)S(1)} %compare_and_fusion.3, pred[8]{0:T(512)(128)(4,1)S(1)} %get-tuple-element.5, ...), kind=kOutput, calls=%fused_computation.8 | convolution fusion | flops 1612709888 | bytes 8912912 | tf_op jit(solution)/shard_map/qab,bc->qac/dot_general | solution.py:99
  483.3 6.0 %copy.41 = f32[8,1,256,1,256]{4,3,2,1,0:T(1,128)} copy(f32[8,1,256,1,256]{2,4,0,3,1:T(8,128)} %fusion) | data formatting | bytes 4194304 | tf_op jit(solution)/shard_map/reshape | solution.py:105
  (56 shorter events, 1.4 us)
Async XLA Ops:
  6.5 10.3 %copy-start = (f32[8,1,256,256]{3,2,1,0:T(8,128)S(1)}, f32[8,1,256,256]{3,2,1,0:T(8,128)}, u32[]{:S(2)}) copy-start(f32[8,1,256,256]{3,2,1,0:T(8,128)} %param.13) | copy-start | bytes 6291460
  6.5 116.6 %all-reduce.5.cloned.1.call-start = ((), (), s32[]{:S(2)}) async-start(), calls=%async_computation | async-start | bytes 4194304 | tf_op jit(solution)/shard_map/psum | solution.py:101
  6.5 4.6 copy-start.8
  9.7 7.6 %copy-start.9 = (f32[8,1,256]{2,1,0:T(1,128)S(1)}, f32[8,1,256]{2,1,0:T(1,128)}, u32[]{:S(2)}) copy-start(f32[8,1,256]{2,1,0:T(1,128)} %param.14) | copy-start | bytes 24580
  9.7 7.6 %copy-start.10 = (f32[1,256,256]{2,1,0:T(8,128)S(1)}, f32[1,256,256]{2,1,0:T(8,128)}, u32[]{:S(2)}) copy-start(f32[1,256,256]{2,1,0:T(8,128)} %param.15) | copy-start | bytes 786436
  9.7 7.6 %copy-start.14 = (f32[1,256]{1,0:T(1,128)S(1)}, f32[1,256]{1,0:T(1,128)}, u32[]{:S(2)}) copy-start(f32[1,256]{1,0:T(1,128)} %param.17) | copy-start | bytes 3076
  9.7 69.3 %collective-permute-start = (f32[8,256,256]{2,1,0:T(8,128)}, f32[8,256,256]{2,1,0:T(8,128)}, u32[]{:S(2)}, u32[]{:S(2)}) collective-permute-start(f32[8,256,256]{2,1,0:T(8,128)} %bitcast.130), channel_id=1, source_target_pairs={{1,0},{2,1},{3,2},{4,3},{5,4},{6,5},{7,6},{8,7},{9,8},{10,9},{11,1... | collective-permute-start | bytes 6291464 | tf_op jit(solution)/shard_map/ppermute | solution.py:13
  12.7 6.4 %copy-start.7 = (f32[1,256,256]{2,1,0:T(8,128)S(1)}, f32[1,256,256]{2,1,0:T(8,128)}, u32[]{:S(2)}) copy-start(f32[1,256,256]{2,1,0:T(8,128)} %param.16) | copy-start | bytes 786436
  12.7 61.0 %collective-permute-start.1 = (f32[8,256,256]{2,1,0:T(8,128)}, f32[8,256,256]{2,1,0:T(8,128)}, u32[]{:S(2)}, u32[]{:S(2)}) collective-permute-start(f32[8,256,256]{2,1,0:T(8,128)} %bitcast.129), channel_id=1, source_target_pairs={{0,16},{16,0},{1,17},{17,1},{2,18},{18,2},{3,19},{19,3},{4,20},{20... | collective-permute-start | bytes 6291464 | tf_op jit(solution)/shard_map/ppermute | solution.py:19
  21.4 216.5 %all-reduce.7.cloned.1.call-start = ((), (), s32[]{:S(2)}) async-start(), calls=%async_computation.1 | async-start | bytes 4194304 | tf_op jit(solution)/shard_map/psum | solution.py:101
  123.2 9.0 %copy-start.11 = (f32[1,256,256]{2,1,0:T(8,128)S(1)}, f32[1,256,256]{2,1,0:T(8,128)}, u32[]{:S(2)}) copy-start(f32[1,256,256]{2,1,0:T(8,128)} %param.15) | copy-start | bytes 786436
  130.4 1.4 copy-start.2
  136.2 223.8 %all-reduce.9.cloned.1.call-start = ((), (), s32[]{:S(2)}) async-start(), calls=%async_computation.2 | async-start | bytes 4194304 | tf_op jit(solution)/shard_map/psum | solution.py:101
  136.2 129.0 %collective-permute-start.2 = (f32[8,256,256]{2,1,0:T(8,128)}, f32[8,256,256]{2,1,0:T(8,128)}, u32[]{:S(2)}, u32[]{:S(2)}) collective-permute-start(f32[8,256,256]{2,1,0:T(8,128)} %bitcast.130), channel_id=1, source_target_pairs={{0,1},{1,2},{2,3},{3,4},{4,5},{5,6},{6,7},{7,8},{8,9},{9,10},{10,1... | collective-permute-start | bytes 6291464 | tf_op jit(solution)/shard_map/ppermute | solution.py:13
  237.9 5.9 %copy-start.3 = (f32[8,256,256]{1,2,0:T(8,128)S(1)}, f32[8,256,256]{1,2,0:T(8,128)}, u32[]{:S(2)}) copy-start(f32[8,256,256]{1,2,0:T(8,128)} %copy-done.2) | copy-start | bytes 6291460
  237.9 5.9 %copy-start.6 = (f32[8,1,256,1,256]{4,3,2,1,0:T(1,128)S(1)}, f32[8,1,256,1,256]{4,3,2,1,0:T(1,128)}, u32[]{:S(2)}) copy-start(f32[8,1,256,1,256]{4,3,2,1,0:T(1,128)} %param.9) | copy-start | bytes 6291460
  243.8 5.7 %copy-start.12 = (f32[1,256,256]{2,1,0:T(8,128)S(1)}, f32[1,256,256]{2,1,0:T(8,128)}, u32[]{:S(2)}) copy-start(f32[1,256,256]{2,1,0:T(8,128)} %param.15) | copy-start | bytes 786436
  247.7 1.3 copy-start.1
  253.3 217.3 %all-reduce.11.cloned.1.call-start = ((), (), s32[]{:S(2)}) async-start(), calls=%async_computation.3 | async-start | bytes 4194304 | tf_op jit(solution)/shard_map/psum | solution.py:101
  253.4 223.1 %collective-permute-start.3 = (f32[8,256,256]{2,1,0:T(8,128)}, f32[8,256,256]{2,1,0:T(8,128)}, u32[]{:S(2)}, u32[]{:S(2)}) collective-permute-start(f32[8,256,256]{2,1,0:T(8,128)} %bitcast.130), channel_id=1, source_target_pairs={{0,2},{1,3},{2,4},{3,5},{4,6},{5,7},{6,8},{7,9},{8,10},{9,11},{10,... | collective-permute-start | bytes 6291464 | tf_op jit(solution)/shard_map/ppermute | solution.py:13
  360.0 9.0 %copy-start.13 = (f32[1,256,256]{2,1,0:T(8,128)S(1)}, f32[1,256,256]{2,1,0:T(8,128)}, u32[]{:S(2)}) copy-start(f32[1,256,256]{2,1,0:T(8,128)} %param.15) | copy-start | bytes 786436
  367.2 1.3 copy-start.4
  470.6 5.9 %copy-start.5 = (f32[8,256,256]{1,2,0:T(8,128)S(1)}, f32[8,256,256]{1,2,0:T(8,128)}, u32[]{:S(2)}) copy-start(f32[8,256,256]{1,2,0:T(8,128)} %copy-done.4) | copy-start | bytes 6291460
Sparse Core Ops, SparseCore 0:
  21.5 101.6 all-reduce.4
  136.3 101.5 all-reduce.6
  253.4 106.4 all-reduce.8
  373.0 97.5 all-reduce.10
